TPU v7x, 8 devices: a whole 2x2x1 slice. The times are simulated.
8 devices in a mesh: batch: 1 (over z), src: 2 (over y), graph: 4 (over x, core).
Axes of the slice: x: 2, y: 2, z: 1, core: 2. Of those that a mesh axis runs over, the one named last changes fastest.
Arguments:
- adj: bfloat16 [16384, 16384], P(('batch', 'graph'))
- sources: int32 [512], P(('batch', 'src'))
- level_weight: float32 [11], replicated
Outputs:
- output: float32 [16384], P(('batch', 'graph'))
All inputs are finite; a program needn't handle non-finite values.
Results may differ from a plain program's by a relative error of at most 0.001.
Values are sent between devices in bfloat16 or wider.
A program may use at most 1 GiB of HBM per device.

v0:
```python
import jax
import jax.numpy as jnp
from jax import lax
from jax.sharding import PartitionSpec as P

exact_precision = lax.Precision.HIGHEST


def solution(mesh):
    src_devices = mesh.shape["src"]

    def device_program(adj_slab, src_local, level_weight):
        slab_rows, vertex_count = adj_slab.shape
        src_count = src_local.shape[0]
        levels = level_weight.shape[0] + 1
        row_start = lax.axis_index("graph") * slab_rows
        vertex_ids = row_start + lax.broadcasted_iota(jnp.int32, (slab_rows, 1), 0)
        sigma = jnp.where(vertex_ids == src_local[None, :], 1.0, 0.0).astype(jnp.float32)
        seen = sigma
        sigmas = []
        for level in range(levels):
            partial_counts = jnp.einsum("uv,us->vs", adj_slab, sigma, preferred_element_type=jnp.float32, precision=exact_precision)
            summed = lax.psum_scatter(partial_counts, "graph", scatter_dimension=0, tiled=True)
            sigma = summed * (1.0 - seen)
            seen = jnp.maximum(seen, jnp.where(sigma > 0, 1.0, 0.0))
            sigmas.append(sigma)
        delta = jnp.zeros_like(sigma)
        total = jnp.zeros_like(sigma)
        for level in range(levels - 1, 0, -1):
            sig_upper = sigmas[level]
            reached = sig_upper > 0
            weights = jnp.where(reached, (level_weight[level - 1] + delta) / jnp.where(reached, sig_upper, 1.0), 0.0)
            gathered = lax.all_gather(weights, "graph", axis=0, tiled=True)
            pulled = jnp.einsum("uv,vs->us", adj_slab, gathered, preferred_element_type=jnp.float32, precision=exact_precision)
            delta = sigmas[level - 1] * pulled
            total = total + delta
        scale = vertex_count / (src_count * src_devices * levels ** 3)
        return lax.psum(jnp.sum(total, axis=1) * scale, "src")

    return jax.shard_map(device_program, mesh=mesh,
                         in_specs=(P(("batch", "graph"), None), P(("batch", "src")), P(None)),
                         out_specs=P(("batch", "graph")), check_vma=False)
```

profile of v0, /device:TPU:0, one launch (start us, length us, event | category | flops | bytes accessed | tf_op | source)
XLA Modules:
  0.0 5338.8 jit_solution(14376580910284461442)
XLA Ops:
  123.6 121.5 %reduce-scatter.13.cloned.1.call-done = f32[4096,256]{0,1:T(8,128)} async-done(((f32[16384,256]{0,1:T(8,128)}), f32[4096,256]{0,1:T(8,128)}) %reduce-scatter.13.cloned.1.call-update) | async-done | bytes 4194320 | tf_op jit(solution)/shard_map/reduce_scatter | solution.py:23
  245.1 118.8 %convolution_bitcast_fusion.10 = f32[16384,256]{0,1:T(8,128)} fusion(bf16[4096,16384]{1,0:T(8,128)(2,1)} %param.3, f32[4096,256]{0,1:T(8,128)} %reduce-scatter.13.cloned.1.call-done, s32[4096]{0:T(1024)S(1)} %iota_add_fusion, s32[256]{0:T(256)S(1)} %copy-done.3), kind=kOutput, calls=%fused_computation.10 | convolution fusion | flops 206162624512 | bytes 155206656 | tf_op jit(solution)/shard_map/uv,us->vs/dot_general | solution.py:22
  482.8 126.8 %convolution_bitcast_fusion.9 = f32[16384,256]{0,1:T(8,128)} fusion(bf16[4096,16384]{1,0:T(8,128)(2,1)} %param.3, f32[4096,256]{0,1:T(8,128)} %reduce-scatter.15.cloned.1.call-done, pred[4096,256]{0,1:T(32,128)(4,1)S(1)} %fusion.28, s32[4096]{0:T(1024)S(1)} %iota_add_fusion, s32[256]{0:T(256)S(1)} %copy-done.3), kind=kOutput, calls=%fused_computation.9 | convolution fusion | flops 206164721664 | bytes 156255232 | tf_op jit(solution)/shard_map/uv,us->vs/dot_general | solution.py:22
  610.0 118.6 %reduce-scatter.17.cloned.1.call-done = f32[4096,256]{0,1:T(8,128)} async-done(((f32[16384,256]{0,1:T(8,128)}), f32[4096,256]{0,1:T(8,128)}) %reduce-scatter.17.cloned.1.call-update) | async-done | bytes 4194320 | tf_op jit(solution)/shard_map/reduce_scatter | solution.py:23
  850.7 118.3 %reduce-scatter.19.cloned.1.call-done = f32[4096,256]{0,1:T(8,128)} async-done(((f32[16384,256]{0,1:T(8,128)}), f32[4096,256]{0,1:T(8,128)}) %reduce-scatter.19.cloned.1.call-update) | async-done | bytes 4194320 | tf_op jit(solution)/shard_map/reduce_scatter | solution.py:23
  969.1 116.5 %convolution_bitcast_fusion.7 = f32[16384,256]{0,1:T(8,128)} fusion(bf16[4096,16384]{1,0:T(8,128)(2,1)} %param.3, f32[4096,256]{0,1:T(8,128)} %reduce-scatter.19.cloned.1.call-done, f32[4096,256]{0,1:T(8,128)} %get-tuple-element.11), kind=kOutput, calls=%fused_computation.7 | convolution fusion | flops 206160527360 | bytes 159383552 | tf_op jit(solution)/shard_map/uv,us->vs/dot_general | solution.py:22
  1085.8 118.6 %reduce-scatter.21.cloned.1.call-done = f32[4096,256]{0,1:T(8,128)} async-done(((f32[16384,256]{0,1:T(8,128)}), f32[4096,256]{0,1:T(8,128)}) %reduce-scatter.21.cloned.1.call-update) | async-done | bytes 4194320 | tf_op jit(solution)/shard_map/reduce_scatter | solution.py:23
  1328.2 118.6 %reduce-scatter.23.cloned.1.call-done = f32[4096,256]{0,1:T(8,128)} async-done(((f32[16384,256]{0,1:T(8,128)}), f32[4096,256]{0,1:T(8,128)}) %reduce-scatter.23.cloned.1.call-update) | async-done | bytes 4194320 | tf_op jit(solution)/shard_map/reduce_scatter | solution.py:23
  1446.8 116.5 %convolution_bitcast_fusion.5 = f32[16384,256]{0,1:T(8,128)} fusion(bf16[4096,16384]{1,0:T(8,128)(2,1)} %param.3, f32[4096,256]{0,1:T(8,128)} %reduce-scatter.23.cloned.1.call-done, f32[4096,256]{0,1:T(8,128)} %get-tuple-element.9), kind=kOutput, calls=%fused_computation.5 | convolution fusion | flops 206160527360 | bytes 159383552 | tf_op jit(solution)/shard_map/uv,us->vs/dot_general | solution.py:22
  1563.6 118.6 %reduce-scatter.25.cloned.1.call-done = f32[4096,256]{0,1:T(8,128)} async-done(((f32[16384,256]{0,1:T(8,128)}), f32[4096,256]{0,1:T(8,128)}) %reduce-scatter.25.cloned.1.call-update) | async-done | bytes 4194320 | tf_op jit(solution)/shard_map/reduce_scatter | solution.py:23
  1806.0 118.4 %reduce-scatter.27.cloned.1.call-done = f32[4096,256]{0,1:T(8,128)} async-done(((f32[16384,256]{0,1:T(8,128)}), f32[4096,256]{0,1:T(8,128)}) %reduce-scatter.27.cloned.1.call-update) | async-done | bytes 4194320 | tf_op jit(solution)/shard_map/reduce_scatter | solution.py:23
  1924.4 116.5 %convolution_bitcast_fusion.3 = f32[16384,256]{0,1:T(8,128)} fusion(bf16[4096,16384]{1,0:T(8,128)(2,1)} %param.3, f32[4096,256]{0,1:T(8,128)} %reduce-scatter.27.cloned.1.call-done, f32[4096,256]{0,1:T(8,128)} %get-tuple-element.7), kind=kOutput, calls=%fused_computation.3 | convolution fusion | flops 206160527360 | bytes 159383552 | tf_op jit(solution)/shard_map/uv,us->vs/dot_general | solution.py:22
  2041.1 118.7 %reduce-scatter.29.cloned.1.call-done = f32[4096,256]{0,1:T(8,128)} async-done(((f32[16384,256]{0,1:T(8,128)}), f32[4096,256]{0,1:T(8,128)}) %reduce-scatter.29.cloned.1.call-update) | async-done | bytes 4194320 | tf_op jit(solution)/shard_map/reduce_scatter | solution.py:23
  2283.5 118.6 %reduce-scatter.31.cloned.1.call-done = f32[4096,256]{0,1:T(8,128)} async-done(((f32[16384,256]{0,1:T(8,128)}), f32[4096,256]{0,1:T(8,128)}) %reduce-scatter.31.cloned.1.call-update) | async-done | bytes 4194320 | tf_op jit(solution)/shard_map/reduce_scatter | solution.py:23
  2402.1 116.5 %convolution_bitcast_fusion.1 = f32[16384,256]{0,1:T(8,128)} fusion(bf16[4096,16384]{1,0:T(8,128)(2,1)} %param.3, f32[4096,256]{0,1:T(8,128)} %reduce-scatter.31.cloned.1.call-done, f32[4096,256]{0,1:T(8,128)} %get-tuple-element.5), kind=kOutput, calls=%fused_computation.1 | convolution fusion | flops 206160527360 | bytes 159383552 | tf_op jit(solution)/shard_map/uv,us->vs/dot_general | solution.py:22
  2518.9 118.6 %reduce-scatter.33.cloned.1.call-done = f32[4096,256]{0,1:T(8,128)} async-done(((f32[16384,256]{0,1:T(8,128)}), f32[4096,256]{0,1:T(8,128)}) %reduce-scatter.33.cloned.1.call-update) | async-done | bytes 4194320 | tf_op jit(solution)/shard_map/reduce_scatter | solution.py:23
  2759.9 117.5 %reduce-scatter.35.cloned.1.call-done = f32[4096,256]{0,1:T(8,128)} async-done(((f32[16384,256]{0,1:T(8,128)}), f32[4096,256]{0,1:T(8,128)}) %reduce-scatter.35.cloned.1.call-update) | async-done | bytes 4194320 | tf_op jit(solution)/shard_map/reduce_scatter | solution.py:23
  3211.7 116.7 %divide_select_fusion.8 = (f32[4096,256]{0,1:T(8,128)}, f32[4096,256]{0,1:T(8,128)}) fusion(f32[]{:T(128)} %bitcast.16, f32[4096,256]{0,1:T(8,128)} %reduce-scatter.31.cloned.1.call-done, f32[4096,256]{0,1:T(8,128)} %get-tuple-element.5, f32[16384,256]{0,1:T(8,128)} %all-gather.14.cloned.1.call-done, bf16[4096,16384]{1,0:T(8,128)(2,1)} %param.3), kind=kOutput, calls=%fused_computation.67 | convolution fusion | flops 206166818816 | bytes 167772160 | tf_op jit(solution)/shard_map/uv,vs->us/dot_general | solution.py:34
  3653.1 116.9 %divide_select_fusion.6 = (f32[4096,256]{0,1:T(8,128)}, f32[4096,256]{0,1:T(8,128)}) fusion(f32[]{:T(128)} %bitcast.20, f32[4096,256]{0,1:T(8,128)} %reduce-scatter.27.cloned.1.call-done, f32[4096,256]{0,1:T(8,128)} %get-tuple-element.7, f32[16384,256]{0,1:T(8,128)} %all-gather.18.cloned.1.call-done, bf16[4096,16384]{1,0:T(8,128)(2,1)} %param.3), kind=kOutput, calls=%fused_computation.61 | convolution fusion | flops 206166818816 | bytes 167772160 | tf_op jit(solution)/shard_map/uv,vs->us/dot_general | solution.py:34
  3874.3 115.9 %divide_select_fusion.5 = (f32[4096,256]{0,1:T(8,128)}, f32[4096,256]{0,1:T(8,128)}) fusion(f32[4096,256]{0,1:T(8,128)} %copy-done.6, f32[]{:T(128)} %bitcast.22, f32[16384,256]{0,1:T(8,128)} %all-gather.20.cloned.1.call-done, bf16[4096,16384]{1,0:T(8,128)(2,1)} %param.3), kind=kOutput, calls=%fused_computation.58 | convolution fusion | flops 206164721664 | bytes 163577856 | tf_op jit(solution)/shard_map/uv,vs->us/dot_general | solution.py:34
  4094.6 116.9 %divide_select_fusion.4 = (f32[4096,256]{0,1:T(8,128)}, f32[4096,256]{0,1:T(8,128)}) fusion(f32[]{:T(128)} %bitcast.24, f32[4096,256]{0,1:T(8,128)} %reduce-scatter.23.cloned.1.call-done, f32[4096,256]{0,1:T(8,128)} %get-tuple-element.9, f32[16384,256]{0,1:T(8,128)} %all-gather.22.cloned.1.call-done, bf16[4096,16384]{1,0:T(8,128)(2,1)} %param.3), kind=kOutput, calls=%fused_computation.55 | convolution fusion | flops 206166818816 | bytes 167772160 | tf_op jit(solution)/shard_map/uv,vs->us/dot_general | solution.py:34
  4536.2 116.8 %divide_select_fusion.2 = (f32[4096,256]{0,1:T(8,128)}, f32[4096,256]{0,1:T(8,128)}) fusion(f32[]{:T(128)} %bitcast.28, f32[4096,256]{0,1:T(8,128)} %reduce-scatter.19.cloned.1.call-done, f32[4096,256]{0,1:T(8,128)} %get-tuple-element.11, f32[16384,256]{0,1:T(8,128)} %all-gather.26.cloned.1.call-done, bf16[4096,16384]{1,0:T(8,128)(2,1)} %param.3), kind=kOutput, calls=%fused_computation.49 | convolution fusion | flops 206166818816 | bytes 167772160 | tf_op jit(solution)/shard_map/uv,vs->us/dot_general | solution.py:34
  4977.5 117.1 %divide_select_fusion = (f32[4096,256]{0,1:T(8,128)}, f32[4096,256]{0,1:T(8,128)}) fusion(f32[]{:T(128)} %bitcast.32, f32[4096,256]{0,1:T(8,128)} %reduce-scatter.15.cloned.1.call-done, pred[4096,256]{0,1:T(32,128)(4,1)S(1)} %copy-done.9, s32[256]{0:T(256)S(1)} %copy-done.4, s32[4096]{0:T(1024)S(1)} %copy-done.2, ...), kind=kOutput, calls=%fused_computation.43 | convolution fusion | flops 206171013120 | bytes 164643840 | tf_op jit(solution)/shard_map/uv,vs->us/dot_general | solution.py:34
  5199.0 124.0 %fusion.38 = f32[4096]{0:T(1024)S(1)} fusion(f32[16384,256]{0,1:T(8,128)} %all-gather.32.cloned.1.call-done, bf16[4096,16384]{1,0:T(8,128)(2,1)} %param.3, f32[4096,256]{0,1:T(8,128)} %reduce-scatter.13.cloned.1.call-done, s32[256]{0:T(256)S(1)} %copy-done.4, s32[4096]{0:T(1024)S(1)} %copy-done.2, f32[4096,256]{0,1:T(8,128)} %get-tuple-element.43, ...), kind=kOutput, calls=%fused_computation.94 | convolution fusion | flops 206175207424 | bytes 197166080 | tf_op jit(solution)/shard_map/uv,vs->us/dot_general | solution.py:34
  (102 shorter events, 2482.8 us)
Async XLA Ops:
  6.5 238.5 %reduce-scatter.13.cloned.1.call-start = ((), (), s32[]{:S(2)}) async-start(), calls=%async_computation.12 | async-start | bytes 20971520 | tf_op jit(solution)/shard_map/reduce_scatter | solution.py:23
  6.5 722.0 %copy-start.1 = (s32[4096]{0:T(1024)}, s32[4096]{0:T(1024)S(1)}, u32[]{:S(2)}) copy-start(s32[4096]{0:T(1024)S(1)} %iota_add_fusion) | copy-start | bytes 49156
  123.3 359.5 %reduce-scatter.15.cloned.1.call-start = ((), (), s32[]{:S(2)}) async-start(), calls=%async_computation.13 | async-start | bytes 20971520 | tf_op jit(solution)/shard_map/reduce_scatter | solution.py:23
  363.9 364.7 %reduce-scatter.17.cloned.1.call-start = ((), (), s32[]{:S(2)}) async-start(), calls=%async_computation.14 | async-start | bytes 20971520 | tf_op jit(solution)/shard_map/reduce_scatter | solution.py:23
  609.7 359.4 %reduce-scatter.19.cloned.1.call-start = ((), (), s32[]{:S(2)}) async-start(), calls=%async_computation.15 | async-start | bytes 20971520 | tf_op jit(solution)/shard_map/reduce_scatter | solution.py:23
  850.2 354.2 %reduce-scatter.21.cloned.1.call-start = ((), (), s32[]{:S(2)}) async-start(), calls=%async_computation.16 | async-start | bytes 20971520 | tf_op jit(solution)/shard_map/reduce_scatter | solution.py:23
  1085.6 361.2 %reduce-scatter.23.cloned.1.call-start = ((), (), s32[]{:S(2)}) async-start(), calls=%async_computation.17 | async-start | bytes 20971520 | tf_op jit(solution)/shard_map/reduce_scatter | solution.py:23
  1327.9 354.2 %reduce-scatter.25.cloned.1.call-start = ((), (), s32[]{:S(2)}) async-start(), calls=%async_computation.18 | async-start | bytes 20971520 | tf_op jit(solution)/shard_map/reduce_scatter | solution.py:23
  1563.3 361.1 %reduce-scatter.27.cloned.1.call-start = ((), (), s32[]{:S(2)}) async-start(), calls=%async_computation.19 | async-start | bytes 20971520 | tf_op jit(solution)/shard_map/reduce_scatter | solution.py:23
  1805.5 354.3 %reduce-scatter.29.cloned.1.call-start = ((), (), s32[]{:S(2)}) async-start(), calls=%async_computation.20 | async-start | bytes 20971520 | tf_op jit(solution)/shard_map/reduce_scatter | solution.py:23
  2040.9 361.2 %reduce-scatter.31.cloned.1.call-start = ((), (), s32[]{:S(2)}) async-start(), calls=%async_computation.21 | async-start | bytes 20971520 | tf_op jit(solution)/shard_map/reduce_scatter | solution.py:23
  2283.2 354.3 %reduce-scatter.33.cloned.1.call-start = ((), (), s32[]{:S(2)}) async-start(), calls=%async_computation.22 | async-start | bytes 20971520 | tf_op jit(solution)/shard_map/reduce_scatter | solution.py:23
  2518.6 358.8 %reduce-scatter.35.cloned.1.call-start = ((), (), s32[]{:S(2)}) async-start(), calls=%async_computation.23 | async-start | bytes 20971520 | tf_op jit(solution)/shard_map/reduce_scatter | solution.py:23
  2758.6 232.9 %all-gather.12.cloned.1.call-start = ((), (), s32[]{:S(2)}) async-start(), calls=%async_computation.24 | async-start | bytes 20971520 | tf_op jit(solution)/shard_map/all_gather | solution.py:33
  2887.1 324.6 %all-gather.14.cloned.1.call-start = ((), (), s32[]{:S(2)}) async-start(), calls=%async_computation.25 | async-start | bytes 20971520 | tf_op jit(solution)/shard_map/all_gather | solution.py:33
  3107.4 325.4 %all-gather.16.cloned.1.call-start = ((), (), s32[]{:S(2)}) async-start(), calls=%async_computation.26 | async-start | bytes 20971520 | tf_op jit(solution)/shard_map/all_gather | solution.py:33
  3328.5 324.6 %all-gather.18.cloned.1.call-start = ((), (), s32[]{:S(2)}) async-start(), calls=%async_computation.27 | async-start | bytes 20971520 | tf_op jit(solution)/shard_map/all_gather | solution.py:33
  3548.7 325.6 %all-gather.20.cloned.1.call-start = ((), (), s32[]{:S(2)}) async-start(), calls=%async_computation.28 | async-start | bytes 20971520 | tf_op jit(solution)/shard_map/all_gather | solution.py:33
  3770.0 324.6 %all-gather.22.cloned.1.call-start = ((), (), s32[]{:S(2)}) async-start(), calls=%async_computation.29 | async-start | bytes 20971520 | tf_op jit(solution)/shard_map/all_gather | solution.py:33
  3990.3 325.6 %all-gather.24.cloned.1.call-start = ((), (), s32[]{:S(2)}) async-start(), calls=%async_computation.30 | async-start | bytes 20971520 | tf_op jit(solution)/shard_map/all_gather | solution.py:33
  4211.6 324.6 %all-gather.26.cloned.1.call-start = ((), (), s32[]{:S(2)}) async-start(), calls=%async_computation.31 | async-start | bytes 20971520 | tf_op jit(solution)/shard_map/all_gather | solution.py:33
  4431.8 325.5 %all-gather.28.cloned.1.call-start = ((), (), s32[]{:S(2)}) async-start(), calls=%async_computation.32 | async-start | bytes 20971520 | tf_op jit(solution)/shard_map/all_gather | solution.py:33
  4653.0 324.5 %all-gather.30.cloned.1.call-start = ((), (), s32[]{:S(2)}) async-start(), calls=%async_computation.33 | async-start | bytes 20971520 | tf_op jit(solution)/shard_map/all_gather | solution.py:33
  4873.2 325.8 %all-gather.32.cloned.1.call-start = ((), (), s32[]{:S(2)}) async-start(), calls=%async_computation.34 | async-start | bytes 20971520 | tf_op jit(solution)/shard_map/all_gather | solution.py:33
  (10 other events, 685.8 us)
Sparse Core Ops, SparseCore 0:
  123.5 121.5 reduce-scatter.12
  364.0 118.7 reduce-scatter.14
  609.8 118.7 reduce-scatter.16
  850.3 118.7 reduce-scatter.18
  1085.7 118.6 reduce-scatter.20
  1328.0 118.7 reduce-scatter.22
  1563.4 118.7 reduce-scatter.24
  1805.6 118.7 reduce-scatter.26
  2041.0 118.7 reduce-scatter.28
  2283.3 118.7 reduce-scatter.30
  2518.8 118.7 reduce-scatter.32
  2758.7 118.7 reduce-scatter.34
  2887.2 104.1 all-gather.11
  3107.5 104.1 all-gather.13
  3328.6 104.1 all-gather.15
  3548.9 104.1 all-gather.17
  3770.1 104.1 all-gather.19
  3990.4 104.1 all-gather.21
  4211.7 104.1 all-gather.23
  4431.9 104.1 all-gather.25
  4653.1 104.1 all-gather.27
  4873.3 104.1 all-gather.29
  5094.8 104.1 all-gather.31
where the time goes:
time: 5340 us
  matrix products  2680 us (50%)
  waiting for transfers between devices  2570 us (48%)
  other arithmetic  55 us (1%)
    reduce_scatter x12, waiting for transfers between devices, device_program(): lax.psum_scatter(partial_counts, 'graph', scatter_dimension=0, tiled=True)  1420 us
    dot_general x12, matrix products, device_program(): jnp.einsum('uv,us->vs', adj_slab, sigma, preferred_element_type=jnp.float...  1390 us
    dot_general x11, matrix products, device_program(): jnp.einsum('uv,vs->us', adj_slab, gathered, preferred_element_type=jnp.fl...  1290 us
    all_gather x11, waiting for transfers between devices, device_program(): gathered = lax.all_gather(weights, 'graph', axis=0, tiled=True)  1140 us
  transfers between devices with their start and end apart: 23, of which 23 were waited for; matrix products, arithmetic and copies ran while one was open for 0% of the time, Pallas kernels for 0%

commit v1 on v0

v1 whole, which is shorter than its diff:
```python
import functools

import jax
import jax.numpy as jnp
from jax import lax
from jax.experimental import pallas as pl
from jax.experimental.pallas import tpu as pltpu
from jax.sharding import PartitionSpec as P

MESH = pl.DeviceIdType.MESH
exact_precision = lax.Precision.HIGHEST
f32 = jnp.float32

LANES = 128
WIDE = 256
DEG = 8
EMPTY = -2.0
FULL = 32767.0
HALF = 64
SLOTS = 8
WINDOW = 64
CAP = 1024
TURN = (((1,), (1,)), ((), ()))


def extract_kernel(half_ref, a_ref, o_ref, tops_ref, seen_ref, *, group=4, step=8):
    block, vertices = a_ref.shape
    chunks = vertices // WIDE
    height = 8 * group

    def scan_rows(t, carry):
        rows = pl.ds(pl.multiple_of(t * height, height), height)

        def scan_chunks(g, state):
            top, low, seen, value = state
            for k in range(step):
                a = a_ref[rows, pl.ds(pl.multiple_of((g * step + k) * WIDE, WIDE), WIDE)]
                x = a * value
                low = jnp.maximum(low, jnp.minimum(top, x))
                top = jnp.maximum(top, x)
                seen = seen + a
                value = value + 1
            return top, low, seen, value

        zero = jnp.zeros((height, WIDE), jnp.bfloat16)
        top, low, seen, _ = lax.fori_loop(0, chunks // step, scan_chunks, (zero, zero, zero, zero + 1))
        tops_ref[0, rows, :] = top
        tops_ref[1, rows, :] = low
        seen_ref[rows, :] = seen
        return carry

    lax.fori_loop(0, block // height, scan_rows, 0)

    ones = jnp.ones((8, WIDE), jnp.bfloat16)
    degree = lax.dot_general(ones, seen_ref[...], TURN, preferred_element_type=jnp.float32)
    crowd = jnp.max(seen_ref[...].astype(jnp.float32)) > 2.0
    simple = jnp.logical_and(jnp.logical_not(crowd), jnp.max(degree) <= DEG // 2)

    @pl.when(crowd)
    def _():
        def scan_chunk(c, carry):
            a = a_ref[:, pl.ds(pl.multiple_of(c * WIDE, WIDE), WIDE)]
            x = a.astype(jnp.float32) * (c + 1).astype(jnp.float32)
            for s in range(DEG):
                top = tops_ref[s].astype(jnp.float32)
                tops_ref[s] = jnp.maximum(top, x).astype(jnp.bfloat16)
                x = jnp.minimum(top, x)
            return carry

        tops_ref[...] = jnp.zeros_like(tops_ref)
        lax.fori_loop(0, chunks, scan_chunk, 0)

    @pl.when(jnp.logical_not(crowd))
    def _():
        tops_ref[2:] = jnp.zeros((DEG - 2, block, WIDE), jnp.bfloat16)

    row_i = lax.broadcasted_iota(jnp.int32, (WIDE, WIDE), 0)
    col_i = lax.broadcasted_iota(jnp.int32, (WIDE, WIDE), 1)
    eye = jnp.where(row_i == col_i, 1.0, 0.0).astype(jnp.bfloat16)
    lane_id = lax.broadcasted_iota(jnp.int32, (8, block), 0).astype(jnp.float32)

    def place(plane, lists):
        flipped = lax.dot_general(eye, tops_ref[plane], TURN, preferred_element_type=jnp.float32)
        lists = list(lists)
        for g in range(WIDE // 8):
            c = flipped[g * 8:(g + 1) * 8]
            x = jnp.where(c > 0, c * WIDE + (lane_id + float(g * 8 - WIDE)), EMPTY)
            for s in range(len(lists)):
                hi = jnp.maximum(lists[s], x)
                x = jnp.minimum(lists[s], x)
                lists[s] = hi
        return lists

    def merge(lists):
        size = len(lists)
        for shift in (4, 2, 1):
            other = [pltpu.roll(v, shift, 0) for v in lists]
            lists = [jnp.maximum(lists[s], other[size - 1 - s]) for s in range(size)]
            gap = size // 2
            while gap:
                for s in range(size):
                    if not s & gap:
                        lists[s], lists[s + gap] = jnp.maximum(lists[s], lists[s + gap]), jnp.minimum(lists[s], lists[s + gap])
                gap //= 2
        sub = lax.broadcasted_iota(jnp.int32, (8, block), 0)
        out = jnp.full((8, block), EMPTY, jnp.float32)
        for s in range(size):
            out = jnp.where(sub == s, lists[s], out)
        return out

    empty = jnp.full((8, block), EMPTY, jnp.float32)

    @pl.when(simple)
    def _():
        lists = [empty] * (DEG // 2)
        for plane in range(2):
            lists = place(plane, lists)
        o_ref[...] = merge(lists)

    @pl.when(jnp.logical_not(simple))
    def _():
        lists = lax.fori_loop(0, DEG, lambda plane, lists: tuple(place(plane, lists)), (empty,) * DEG)
        o_ref[...] = jnp.where(degree > DEG, FULL, merge(list(lists)))


def extract(adj_slab, half, rows, block=128, **kw):
    vertices = adj_slab.shape[1]
    steps = rows // block
    return pl.pallas_call(
        functools.partial(extract_kernel, **kw),
        grid_spec=pltpu.PrefetchScalarGridSpec(
            num_scalar_prefetch=1,
            grid=(steps,),
            in_specs=[pl.BlockSpec((block, vertices), lambda i, h: (h[0] * steps + i, 0))],
            out_specs=pl.BlockSpec((8, block), lambda i, h: (0, i)),
            scratch_shapes=[pltpu.VMEM((DEG, block, WIDE), jnp.bfloat16), pltpu.VMEM((block, WIDE), jnp.bfloat16)],
        ),
        out_shape=jax.ShapeDtypeStruct((DEG, rows), jnp.float32),
        name="extract",
    )(half, adj_slab)


def walk_kernel(lists_ref, src_ref, weight_ref, out_ref,
                table, queue, sigma, ratio, delta, cand, ids, near, bins, ids_s, meta, sem, *, levels, vertices, scale):
    parts, _, width = lists_ref.shape
    dummy = vertices
    lane = lax.broadcasted_iota(jnp.int32, (8, LANES), 1)
    sub = lax.broadcasted_iota(jnp.int32, (8, LANES), 0)
    upper = lane >= HALF
    lane_row = lax.broadcasted_iota(jnp.int32, (1, LANES), 1)
    group_odd = ((lane_row // 32) % 2) == 1
    lane32 = lane_row % 32

    srow = lax.broadcasted_iota(jnp.int32, (2 * DEG, LANES), 0)
    slane = lax.broadcasted_iota(jnp.int32, (2 * DEG, LANES), 1)

    def spread(quad):
        mine = (srow % DEG) == (slane // 32 + 4 * quad)
        return jnp.where(mine, jnp.where(srow < DEG, float(LANES), 1.0), 0.0).astype(jnp.bfloat16)

    def fill(quad):
        pick = spread(quad)
        blocks = width // LANES

        def body(b, most):
            for k in range(4):
                bb = b * 4 + k
                d, c = bb // blocks, bb % blocks
                x = lists_ref[d, :, pl.ds(pl.multiple_of(c * LANES, LANES), LANES)]
                hi = jnp.floor(x * (1.0 / LANES))
                lo = x - hi * LANES
                both = jnp.concatenate([hi, lo], axis=0).astype(jnp.bfloat16)
                rows = lax.dot_general(both, pick, (((0,), (0,)), ((), ())), preferred_element_type=f32)
                table[quad, pl.ds(pl.multiple_of(bb * LANES, LANES), LANES), :] = rows
                most = jnp.maximum(most, x)
            return most

        most = lax.fori_loop(0, parts * blocks // 4, body, jnp.full((DEG, LANES), EMPTY, f32))
        table[quad, vertices:, :] = jnp.full((8, LANES), EMPTY, f32)
        return most

    most = fill(0)
    top = jnp.max(most)
    wide = jnp.max(jnp.where(sub >= 4, most, EMPTY)) >= 0
    quads = jnp.where(wide, 2, 1)

    @pl.when(wide)
    def _():
        fill(1)

    bad = top > vertices
    meta[2, 0] = bad.astype(jnp.int32)

    rows_all = queue.shape[0]

    def clear(t, carry):
        rows = pl.ds(pl.multiple_of(t * 8, 8), 8)
        queue[rows, :] = jnp.full((8, LANES), -1.0, f32)
        sigma[rows, :] = jnp.zeros((8, LANES), f32)
        delta[rows, :] = jnp.zeros((8, LANES), f32)
        ids[rows, :] = jnp.full((8, LANES), dummy, jnp.int32)
        return carry

    lax.fori_loop(0, rows_all // 8, clear, 0)
    bins[...] = jnp.zeros_like(bins)

    def window_rows(base, group):
        return [pl.ds(pl.multiple_of(base + group * WINDOW + 8 * t, 8), 8) for t in range(WINDOW // 8)]

    def gather(slot, row, quad):
        acc = [jnp.full((1, LANES), EMPTY, f32)] * 2
        for j in range(32):
            hit = lane32 == j
            for b in range(2):
                v = ids_s[slot, b * 32 + j]
                acc[b] = jnp.where(hit, table[quad, pl.ds(v, 1), :], acc[b])
        c0 = jnp.where(group_odd, acc[1], acc[0])
        c1 = pltpu.roll(jnp.where(group_odd, acc[0], acc[1]), LANES - 32, 1)
        cand[2 * quad, pl.ds(row, 1), :] = c0
        cand[2 * quad + 1, pl.ds(row, 1), :] = c1

    def bits(x):
        return jnp.where(x, 1, 0)

    def place(c0, c1, near0, near1, tail):
        c0r, c1r = pltpu.roll(c0, HALF, 1), pltpu.roll(c1, HALF, 1)
        both = near0 + 2 * near1
        for shift in (4, 2, 1):
            both = both | pltpu.roll(both, shift, 0)
        both = both | bits(c0 < 0) | (2 * bits(c1 < 0))
        other = pltpu.roll(both, HALF, 1)
        n0, n1 = 1 - (both & 1), 1 - (both >> 1)
        r0, r1 = 1 - (other & 1), 1 - (other >> 1)
        mid = tail + n0 + r0
        d0 = jnp.where(n0 > 0, tail + jnp.where(upper, r0, 0), -1)
        e0 = jnp.where(r0 > 0, tail + jnp.where(upper, 0, n0), -1)
        d1 = jnp.where(n1 > 0, mid + jnp.where(upper, r1, 0), -1)
        e1 = jnp.where(r1 > 0, mid + jnp.where(upper, 0, n1), -1)
        return c0r, c1r, d0, e0, d1, e1, mid + n1 + r1

    def look(c0, c1, q, s, sig, near0, near1):
        m0, m1 = q == c0, q == c1
        return (jnp.where(m0, 1, near0), jnp.where(m1, 1, near1), jnp.where(m0 | m1, s + sig, s))

    def put(pos, q, s, sig, c0, c1, c0r, c1r, d0, e0, d1, e1):
        a, b, c, d = pos == d0, pos == e0, pos == d1, pos == e1
        q = jnp.where(a, c0, jnp.where(b, c0r, jnp.where(c, c1, jnp.where(d, c1r, q))))
        return q, jnp.where(a | c, sig, s)

    def wide_row(ref, row):
        return jnp.broadcast_to(ref[pl.ds(row, 1), :], (8, LANES))

    def wide_cand(which, row):
        return jnp.broadcast_to(cand[which, pl.ds(row, 1), :], (8, LANES))

    def level_step(level, carry):
        base, count = meta[0, level], meta[1, level]
        following = base + (count + 7) // 8 * 8

        def chunk_step(ch, tail):
            first = base + ch * WINDOW
            copy = pltpu.make_async_copy(ids.at[pl.ds(pl.multiple_of(first, 8), WINDOW)], ids_s, sem)
            copy.start()
            copy.wait()
            here = jnp.minimum(count - ch * WINDOW, WINDOW)

            def quad_step(quad, tail):
                for i in range(SLOTS):
                    gather(i, first + i, quad)

                def batch_step(bt, tail):
                    row = first + bt * SLOTS

                    cs = [wide_cand(2 * quad + h, row + i) for i in range(SLOTS) for h in range(2)]

                    def prefix(t, marks):
                        marks = list(marks)
                        for rows in window_rows(0, t):
                            q = queue[rows, :]
                            for m in range(2 * SLOTS):
                                marks[m] = jnp.where(q == cs[m], 1, marks[m])
                        return tuple(marks)

                    marks = lax.fori_loop(0, (following + WINDOW - 1) // WINDOW, prefix,
                                          (jnp.zeros((8, LANES), jnp.int32),) * (2 * SLOTS))
                    for m in range(2 * SLOTS):
                        near[m] = marks[m]

                    slots = window_rows(jnp.minimum(following, CAP), 0)
                    qs = [queue[r, :] for r in slots]
                    ss = [sigma[r, :] for r in slots]
                    newtail = tail
                    for i in range(SLOTS):
                        gather(jnp.minimum(bt * SLOTS + SLOTS + i, WINDOW - 1), row + SLOTS + i, quad)
                        c0, c1 = wide_cand(2 * quad, row + i), wide_cand(2 * quad + 1, row + i)
                        sig = wide_row(sigma, row + i)
                        n0, n1 = near[2 * i], near[2 * i + 1]
                        for t in range(WINDOW // 8):
                            n0, n1, ss[t] = look(c0, c1, qs[t], ss[t], sig, n0, n1)
                        c0r, c1r, d0, e0, d1, e1, newtail = place(c0, c1, n0, n1, newtail)
                        for t in range(WINDOW // 8):
                            qs[t], ss[t] = put(sub + 8 * t, qs[t], ss[t], sig, c0, c1, c0r, c1r, d0, e0, d1, e1)
                    length = jnp.max(newtail)
                    short = jnp.logical_and(length <= WINDOW, following <= CAP)

                    @pl.when(short)
                    def _():
                        for t, r in enumerate(slots):
                            queue[r, :] = qs[t]
                            sigma[r, :] = ss[t]

                    def long_batch(tail):
                        groups = (length + WINDOW - 1) // WINDOW
                        fits = following + groups * WINDOW <= CAP
                        groups = jnp.where(fits, groups, 0)

                        @pl.when(jnp.logical_not(fits))
                        def _():
                            meta[2, 0] = 1

                        def slot_step(i, tail):
                            c0, c1 = wide_cand(2 * quad, row + i), wide_cand(2 * quad + 1, row + i)
                            sig = wide_row(sigma, row + i)

                            def seek(g, marks):
                                n0, n1 = marks
                                for r in window_rows(following, g):
                                    n0, n1, sigma[r, :] = look(c0, c1, queue[r, :], sigma[r, :], sig, n0, n1)
                                return n0, n1

                            n0, n1 = lax.fori_loop(0, groups, seek, (near[2 * i], near[2 * i + 1]))
                            c0r, c1r, d0, e0, d1, e1, tail = place(c0, c1, n0, n1, tail)

                            def insert(g, carry):
                                for t, r in enumerate(window_rows(following, g)):
                                    queue[r, :], sigma[r, :] = put(sub + (g * WINDOW + 8 * t), queue[r, :], sigma[r, :], sig,
                                                                   c0, c1, c0r, c1r, d0, e0, d1, e1)
                                return carry

                            lax.fori_loop(0, groups, insert, 0)
                            return tail

                        return lax.fori_loop(0, SLOTS, slot_step, tail)

                    return lax.cond(short, lambda t: newtail, long_batch, tail)

                return lax.fori_loop(0, (here + SLOTS - 1) // SLOTS, batch_step, tail)

            return lax.fori_loop(0, quads, quad_step, tail)

        tail = lax.fori_loop(0, (count + WINDOW - 1) // WINDOW, chunk_step, jnp.zeros((8, LANES), jnp.int32))
        found = jnp.where(meta[2, 0] == 0, jnp.max(tail), 0)
        meta[0, level + 1] = following
        meta[1, level + 1] = found

        def settle(g, carry):
            for r in window_rows(following, g):
                q = queue[r, :]
                ids[r, :] = jnp.where(q < 0, dummy, q.astype(jnp.int32))
            for r in window_rows(following, g):
                s = sigma[r, :]
                sigma[r, :] = s + pltpu.roll(s, HALF, 1)
            return carry

        lax.fori_loop(0, (found + WINDOW - 1) // WINDOW, settle, 0)
        return carry

    @pl.when(jnp.logical_not(bad))
    def _():
        queue[0:1, :] = src_ref[...]
        sigma[0:1, :] = jnp.ones((1, LANES), f32)
        ids[0:1, :] = src_ref[...].astype(jnp.int32)
        meta[0, 0] = 0
        meta[1, 0] = 1
        lax.fori_loop(0, levels, level_step, 0)

    good = meta[2, 0] == 0

    @pl.when(good)
    def _():
        last = meta[0, levels]
        g_last = weight_ref[levels - 2]

        def seed(g, carry):
            for r in window_rows(last, g):
                s = sigma[r, :]
                ratio[r, :] = jnp.where(s > 0, g_last / jnp.where(s > 0, s, 1.0), 0.0)
            return carry

        lax.fori_loop(0, (meta[1, levels] + WINDOW - 1) // WINDOW, seed, 0)

        def back_step(k, carry):
            level = levels - 1 - k
            base, count = meta[0, level], meta[1, level]
            nbase, ncount = meta[0, level + 1], meta[1, level + 1]
            g_here = weight_ref[jnp.maximum(level - 2, 0)]

            def batch_step(bt, carry):
                row = pl.multiple_of(base + bt * SLOTS, 8)

                def pull(m, acc):
                    quad, g = m % quads, m // quads
                    acc = list(acc)
                    slots = window_rows(nbase, g)
                    qs = [queue[r, :] for r in slots]
                    ws = [ratio[r, :] for r in slots]
                    for i in range(SLOTS):
                        c0, c1 = wide_cand(2 * quad, row + i), wide_cand(2 * quad + 1, row + i)
                        for t in range(WINDOW // 8):
                            acc[i] = acc[i] + jnp.where((qs[t] == c0) | (qs[t] == c1), ws[t], 0.0)
                    return tuple(acc)

                acc = lax.fori_loop(0, quads * ((ncount + WINDOW - 1) // WINDOW), pull,
                                    (jnp.zeros((8, LANES), f32),) * SLOTS)
                pulled = jnp.concatenate([jnp.sum(a, axis=0, keepdims=True) for a in acc], axis=0)
                pulled = pulled + pltpu.roll(pulled, HALF, 1)
                here = pl.ds(row, SLOTS)
                s = sigma[here, :]
                d = s * pulled
                delta[here, :] = d
                ratio[here, :] = jnp.where(s > 0, (g_here + d) / jnp.where(s > 0, s, 1.0), 0.0)
                return carry

            lax.fori_loop(0, (count + SLOTS - 1) // SLOTS, batch_step, 0)
            return carry

        lax.fori_loop(0, levels - 1, back_step, 0)

        tall = lax.broadcasted_iota(jnp.int32, (LANES, 2 * LANES), 0).astype(f32)
        start = meta[0, 1]

        def tally(t, carry):
            a = pl.ds(pl.multiple_of(start + t * 16, 8), 8)
            b = pl.ds(pl.multiple_of(start + t * 16 + 8, 8), 8)
            v = jnp.where(upper, queue[b, :], queue[a, :])
            d = jnp.where(upper, delta[b, :], delta[a, :])
            hi = jnp.floor(v * (1.0 / LANES))
            lo = v - hi * LANES
            d_hi = d.astype(jnp.bfloat16).astype(f32)
            d_mid = (d - d_hi).astype(jnp.bfloat16).astype(f32)
            d_lo = d - d_hi - d_mid
            for p in range(0, 8, 2):
                def pair(x):
                    return jnp.concatenate([x[p:p + 1], x[p + 1:p + 2]], axis=1)
                rowhot = jnp.where(tall == pair(hi), 1.0, 0.0).astype(jnp.bfloat16)
                match = tall == pair(lo)
                colhot = jnp.concatenate([jnp.where(match, pair(x), 0.0).astype(jnp.bfloat16) for x in (d_hi, d_mid, d_lo)], axis=0)
                bins[...] += lax.dot_general(rowhot, colhot, TURN, preferred_element_type=f32)
            return carry

        lax.fori_loop(0, (last - start + 15) // 16, tally, 0)

    blocks = out_ref.shape[0]
    high = LANES // blocks
    total = (bins[:, :LANES] + bins[:, LANES:2 * LANES] + bins[:, 2 * LANES:]) * scale
    flag = jnp.where(good, 0.0, 1.0)
    for b in range(blocks):
        out_ref[b, 0:high, :] = total[b * high:(b + 1) * high]
        out_ref[b, high:, :] = jnp.full((8, LANES), flag, f32)


def walk(lists, src_row, weights, *, blocks, vertices, scale):
    levels = weights.shape[0] + 1
    rows = CAP + WINDOW + 2 * SLOTS
    high = LANES // blocks + 8
    vm = pltpu.VMEM
    return pl.pallas_call(
        functools.partial(walk_kernel, levels=levels, vertices=vertices, scale=scale),
        in_specs=[pl.BlockSpec(memory_space=pltpu.VMEM), pl.BlockSpec(memory_space=pltpu.VMEM), pl.BlockSpec(memory_space=pltpu.SMEM)],
        out_specs=pl.BlockSpec(memory_space=pltpu.VMEM),
        out_shape=jax.ShapeDtypeStruct((blocks, high, LANES), f32),
        scratch_shapes=[
            vm((2, vertices + 8, LANES), f32),
            vm((rows, LANES), f32), vm((rows, LANES), f32), vm((rows, LANES), f32), vm((rows, LANES), f32),
            vm((4, rows, LANES), f32), vm((rows, LANES), jnp.int32),
            vm((2 * SLOTS, 8, LANES), jnp.int32), vm((LANES, 3 * LANES), f32),
            pltpu.SMEM((WINDOW, LANES), jnp.int32), pltpu.SMEM((3, 16), jnp.int32), pltpu.SemaphoreType.DMA,
        ],
        compiler_params=pltpu.CompilerParams(vmem_limit_bytes=48 * 1024 * 1024),
        name="walk",
    )(lists, src_row, weights)


def everyone(src, graph):
    return [(y, g) for y in range(src) for g in range(graph)]


def meet(peers):
    barrier = pltpu.get_barrier_semaphore()
    for y, g in peers:
        pl.semaphore_signal(barrier, inc=1, device_id={"src": y, "graph": g}, device_id_type=MESH)
    pl.semaphore_wait(barrier, len(peers))


def share_kernel(src, graph, x_ref, o_ref, own_sem, send_sem, recv_sem):
    y, g = lax.axis_index("src"), lax.axis_index("graph")
    others = [((y + i) % src, (g + k) % graph) for i, k in everyone(src, graph)][1:]
    meet(others)
    mine = g * src + y
    own = pltpu.make_async_copy(x_ref, o_ref.at[mine], own_sem)
    own.start()
    copies = []
    for n, (py, pg) in enumerate(others):
        copies.append(pltpu.make_async_remote_copy(
            src_ref=x_ref, dst_ref=o_ref.at[mine], send_sem=send_sem.at[n], recv_sem=recv_sem.at[n],
            device_id={"src": py, "graph": pg}, device_id_type=MESH))
        copies[-1].start()
    own.wait()
    for c in copies:
        c.wait()


def share(x, src, graph):
    n = src * graph
    return pl.pallas_call(
        functools.partial(share_kernel, src, graph),
        in_specs=[pl.BlockSpec(memory_space=pltpu.VMEM)],
        out_specs=pl.BlockSpec(memory_space=pltpu.VMEM),
        out_shape=jax.ShapeDtypeStruct((n,) + x.shape, x.dtype),
        scratch_shapes=[pltpu.SemaphoreType.DMA, pltpu.SemaphoreType.DMA((n - 1,)), pltpu.SemaphoreType.DMA((n - 1,))],
        compiler_params=pltpu.CompilerParams(collective_id=0, has_side_effects=True),
        name="share",
    )(x)


def total_kernel(src, graph, x_ref, o_ref, got, own_sem, send_sem, recv_sem):
    y, g = lax.axis_index("src"), lax.axis_index("graph")
    others = [((y + i) % src, (g + k) % graph) for i, k in everyone(src, graph)][1:]
    meet(others)
    mine = g * src + y
    own = pltpu.make_async_copy(x_ref.at[g], got.at[mine], own_sem)
    own.start()
    copies = []
    for n, (py, pg) in enumerate(others):
        copies.append(pltpu.make_async_remote_copy(
            src_ref=x_ref.at[pg], dst_ref=got.at[mine], send_sem=send_sem.at[n], recv_sem=recv_sem.at[n],
            device_id={"src": py, "graph": pg}, device_id_type=MESH))
        copies[-1].start()
    own.wait()
    for c in copies:
        c.wait()
    acc = got[0]
    for n in range(1, src * graph):
        acc = acc + got[n]
    o_ref[...] = acc


def total(x, src, graph):
    n = src * graph
    return pl.pallas_call(
        functools.partial(total_kernel, src, graph),
        in_specs=[pl.BlockSpec(memory_space=pltpu.VMEM)],
        out_specs=pl.BlockSpec(memory_space=pltpu.VMEM),
        out_shape=jax.ShapeDtypeStruct(x.shape[1:], x.dtype),
        scratch_shapes=[pltpu.VMEM((n,) + x.shape[1:], x.dtype), pltpu.SemaphoreType.DMA,
                        pltpu.SemaphoreType.DMA((n - 1,)), pltpu.SemaphoreType.DMA((n - 1,))],
        compiler_params=pltpu.CompilerParams(collective_id=1, has_side_effects=True),
        name="total",
    )(x)


def dense(adj_slab, src_local, level_weight, src, graph):
    slab_rows, vertex_count = adj_slab.shape
    src_count = src_local.shape[0]
    levels = level_weight.shape[0] + 1
    row_start = lax.axis_index("graph") * slab_rows
    vertex_ids = row_start + lax.broadcasted_iota(jnp.int32, (slab_rows, 1), 0)
    first = jnp.where(vertex_ids == src_local[None, :], 1.0, 0.0).astype(f32)

    def forward(carry, unused):
        sigma, seen = carry
        partial = jnp.einsum("uv,us->vs", adj_slab, sigma, preferred_element_type=f32, precision=exact_precision)
        parts = lax.all_to_all(partial.reshape(graph, slab_rows, src_count), "graph", 0, 0)
        sigma = jnp.sum(parts, axis=0) * (1.0 - seen)
        seen = jnp.maximum(seen, jnp.where(sigma > 0, 1.0, 0.0))
        return (sigma, seen), sigma

    _, sigmas = lax.scan(forward, (first, first), None, length=levels)

    def backward(carry, xs):
        delta, acc = carry
        upper, lower, weight = xs
        reached = upper > 0
        ratio = jnp.where(reached, (weight + delta) / jnp.where(reached, upper, 1.0), 0.0)
        gathered = lax.all_to_all(jnp.broadcast_to(ratio[None], (graph,) + ratio.shape), "graph", 0, 0)
        pulled = jnp.einsum("uv,vs->us", adj_slab, gathered.reshape(vertex_count, src_count),
                            preferred_element_type=f32, precision=exact_precision)
        delta = lower * pulled
        return (delta, acc + delta), None

    zero = jnp.zeros_like(first)
    (_, acc), _ = lax.scan(backward, (zero, zero), (sigmas[1:][::-1], sigmas[:-1][::-1], level_weight[::-1]))
    scale = vertex_count / (src_count * src * levels ** 3)
    mine = jnp.sum(acc, axis=1) * scale
    both = lax.all_to_all(jnp.broadcast_to(mine.reshape(1, -1, LANES), (src, slab_rows // LANES, LANES)), "src", 0, 0)
    return jnp.sum(both, axis=0).reshape(slab_rows)


def solution(mesh):
    src, graph = mesh.shape["src"], mesh.shape["graph"]

    def device_program(adj_slab, src_local, level_weight):
        slab_rows, vertex_count = adj_slab.shape
        levels = level_weight.shape[0] + 1
        half = lax.axis_index("src").astype(jnp.int32).reshape(1)
        lists = share(extract(adj_slab, half, slab_rows // src), src, graph)
        mine = lax.dynamic_slice(src_local, (lax.axis_index("graph") * HALF,), (HALF,)).astype(f32)
        scale = vertex_count / (HALF * src * graph * levels ** 3)
        parts = walk(lists, jnp.concatenate([mine, mine])[None], level_weight, blocks=graph, vertices=vertex_count, scale=scale)
        summed = total(parts, src, graph)
        high = slab_rows // LANES
        return lax.cond(summed[high, 0] > 0,
                        lambda: dense(adj_slab, src_local, level_weight, src, graph),
                        lambda: summed[:high].reshape(slab_rows))

    return jax.shard_map(device_program, mesh=mesh,
                         in_specs=(P(("batch", "graph"), None), P(("batch", "src")), P(None)),
                         out_specs=P(("batch", "graph")), check_vma=False)
```

time: 5340 us -> 170 us (0.03)
  matrix products: 2680 us -> 0 us
  waiting for transfers between devices: 2570 us -> 0 us
  Pallas kernels: 0 us -> 165 us
  other arithmetic: 55 us -> 0.83 us
    dot_general x23 -> x0, matrix products: 2680 us -> none  [the longest x12 1390 us: device_program(): jnp.einsum('uv,us->vs', adj_slab, sigma, preferred_element_type=jnp.float...]
    reduce_scatter x12 -> x0, waiting for transfers between devices: 1420 us -> none  [device_program(): lax.psum_scatter(partial_counts, 'graph', scatter_dimension=0, tiled=True)]
    all_gather x11 -> x0, waiting for transfers between devices: 1140 us -> none  [device_program(): gathered = lax.all_gather(weights, 'graph', axis=0, tiled=True)]
    pallas_call x0 -> x4, Pallas kernels: none -> 165 us  [the longest x1 102 us: walk(): pl.pallas_call(functools.partial(walk_kernel, levels=levels, vertices=ver...]
  transfers between devices with their start and end apart: 23 -> 0, of which waited for: 23 -> 0; matrix products, arithmetic and copies ran while one was open for 0% -> 0% of each run, Pallas kernels for 0% -> 0%
where the time goes in v1:
time: 170 us
  Pallas kernels  165 us (97%)
  local copies, waits for them, and re-layouts  2.79 us (2%)
    pallas_call x1, Pallas kernels, walk(): pl.pallas_call(functools.partial(walk_kernel, levels=levels, vertices=ver...  102 us
    pallas_call x1, Pallas kernels, extract(): pl.pallas_call(functools.partial(extract_kernel, **kw), grid_spec=pltpu.P...  32.7 us
    pallas_call x1, Pallas kernels, share(): pl.pallas_call(functools.partial(share_kernel, src, graph), in_specs=[pl....  23.7 us
    pallas_call x1, Pallas kernels, total(): pl.pallas_call(functools.partial(total_kernel, src, graph), in_specs=[pl....  6.94 us

profile of v1, /device:TPU:0, one launch (start us, length us, event | category | flops | bytes accessed | tf_op | source)
XLA Modules:
  0.0 169.6 jit_solution(10370845432203165505)
XLA Ops:
  0.0 0.8 dynamic-slice_convert_fusion
  0.8 0.1 maximum_bitcast_fusion.src_ref
  0.8 0.0 copy-start.4
  0.8 0.0 copy-start.3
  0.8 32.7 %extract.1.x_ref = f32[8,2048]{1,0:T(8,128)} custom-call(s32[1]{0:T(128)} %bitcast.5.half_ref, bf16[4096,16384]{1,0:T(8,128)(2,1)} %a_ref.1), custom_call_target="tpu_custom_call" | custom-call | tf_op jit(solution)/shard_map/extract/pallas_call | solution.py:129
  33.6 23.7 %share.1.lists_ref = f32[8,8,2048]{2,1,0:T(8,128)} custom-call(f32[8,2048]{1,0:T(8,128)} %extract.1.x_ref), custom_call_target="tpu_custom_call" | custom-call | tf_op jit(solution)/shard_map/share/pallas_call | solution.py:515
  57.2 0.0 copy-done.4
  57.2 0.0 copy-start
  57.3 1.0 copy-done
  58.3 101.9 %walk.1.x_ref = f32[4,40,128]{2,1,0:T(8,128)S(1)} custom-call(f32[8,8,2048]{2,1,0:T(8,128)S(1)} %copy-done, f32[1,128]{1,0:T(1,128)S(1)} %maximum_bitcast_fusion.src_ref, f32[11]{0:T(128)S(1)} %copy-done.4), custom_call_target="tpu_custom_call" | custom-call | tf_op jit(solution)/shard_map/walk/pallas_call | solution.py:467
  160.2 0.0 copy-start.1
  160.2 0.6 copy-done.1
  160.8 6.9 %total.1 = f32[40,128]{1,0:T(8,128)S(1)} custom-call(f32[4,40,128]{2,1,0:T(8,128)} %copy-done.1), custom_call_target="tpu_custom_call" | custom-call | tf_op jit(solution)/shard_map/total/pallas_call | solution.py:550
  167.8 0.5 slice.12
  168.9 0.0 copy-done.3
  168.9 0.6 conditional.1
  168.9 0.6 slice_bitcast_fusion
Async XLA Ops:
  0.8 56.4 %copy-start.4 = (f32[11]{0:T(128)S(1)}, f32[11]{0:T(128)}, u32[]{:S(2)}) copy-start(f32[11]{0:T(128)} %weight_ref.1) | copy-start | bytes 136
  0.8 168.1 %copy-start.3 = (s32[256]{0:T(256)S(1)}, s32[256]{0:T(256)}, u32[]{:S(2)}) copy-start(s32[256]{0:T(256)} %param.10) | copy-start | bytes 3076
  57.2 1.0 copy-start
  160.2 0.6 copy-start.1

commit v2 on v1

v2 whole, which is shorter than its diff:
```python
import functools

import jax
import jax.numpy as jnp
from jax import lax
from jax.experimental import pallas as pl
from jax.experimental.pallas import tpu as pltpu
from jax.sharding import PartitionSpec as P

MESH = pl.DeviceIdType.MESH
exact_precision = lax.Precision.HIGHEST
f32 = jnp.float32

LANES = 128
WIDE = 256
DEG = 8
EMPTY = -2.0
FULL = 32767.0
TURN = (((1,), (1,)), ((), ()))
BLOCK = 128
READS = 4
HALF = 64
SLOTS = 8
WINDOW = 48
SCAN = 32
CAP = 1024
SPREAD = 1024


def extract_kernel(half_ref, a_ref, o_ref, bufs, top_ref, low_ref, third_ref, seen_ref, planes, flags, sems, *, group=4, step=16):
    rows, vertices = o_ref.shape[1], a_ref.shape[1]
    blocks, chunks = rows // BLOCK, vertices // WIDE
    first = half_ref[0] * rows
    height = 8 * group

    def fetch(i, slot):
        return pltpu.make_async_copy(a_ref.at[pl.ds(pl.multiple_of(first + i * BLOCK, BLOCK), BLOCK)], bufs.at[slot], sems.at[slot])

    row_i = lax.broadcasted_iota(jnp.int32, (WIDE, WIDE), 0)
    col_i = lax.broadcasted_iota(jnp.int32, (WIDE, WIDE), 1)
    eye = jnp.where(row_i == col_i, float(WIDE), 0.0).astype(jnp.bfloat16)
    ones = jnp.ones((8, WIDE), jnp.bfloat16)
    sub = lax.broadcasted_iota(jnp.int32, (8, BLOCK), 0)
    lane_id = sub.astype(f32)
    none = jnp.zeros((8, BLOCK), f32)

    def place(plane, lists):
        lists = list(lists)
        flipped = lax.dot_general(eye, plane, TURN, preferred_element_type=f32)
        for g in range(WIDE // 8):
            x = flipped[g * 8:(g + 1) * 8] + (lane_id + float(g * 8))
            for s in range(len(lists)):
                hi = jnp.maximum(lists[s], x)
                if s < len(lists) - 1:
                    x = jnp.minimum(lists[s], x)
                lists[s] = hi
        return lists

    def sort(lists):
        gap = len(lists) // 2
        while gap:
            for s in range(len(lists)):
                if not s & gap:
                    lists[s], lists[s + gap] = jnp.maximum(lists[s], lists[s + gap]), jnp.minimum(lists[s], lists[s + gap])
            gap //= 2
        return lists

    def over_sublanes(lists):
        size = len(lists)
        for shift in (4, 2, 1):
            other = [pltpu.roll(v, shift, 0) for v in lists]
            lists = sort([jnp.maximum(lists[s], other[size - 1 - s]) for s in range(size)])
        out = jnp.full((8, BLOCK), EMPTY, f32)
        for s in range(size):
            out = jnp.where(sub == s, jnp.where(lists[s] >= WIDE, lists[s] - WIDE, EMPTY), out)
        return out

    for i in range(READS - 1):
        fetch(i, i).start()

    def block_step(i, carry):
        slot = i % READS

        @pl.when(i + READS - 1 < blocks)
        def _():
            fetch(i + READS - 1, (i + READS - 1) % READS).start()

        fetch(i, slot).wait()

        def scan_rows(t, carry):
            here = pl.ds(pl.multiple_of(t * height, height), height)

            def scan_chunks(g, state):
                top, low, seen, sums, value = state
                for k in range(step):
                    a = bufs[slot, here, pl.ds(pl.multiple_of((g * step + k) * WIDE, WIDE), WIDE)]
                    x = a * value
                    low = jnp.maximum(low, jnp.minimum(top, x))
                    top = jnp.maximum(top, x)
                    seen = seen + a
                    sums = sums + x
                    value = value + 1
                return top, low, seen, sums, value

            zero = jnp.zeros((height, WIDE), jnp.bfloat16)
            top, low, seen, sums, _ = lax.fori_loop(0, chunks // step, scan_chunks, (zero, zero, zero, zero, zero + 1))
            top_ref[here, :] = top
            low_ref[here, :] = low
            third_ref[here, :] = (sums - top) - low
            seen_ref[here, :] = seen
            return carry

        lax.fori_loop(0, BLOCK // height, scan_rows, 0)

        seen = seen_ref[...]
        degree = lax.dot_general(ones, seen, TURN, preferred_element_type=f32)
        crowd = seen[0:8]
        for g in range(1, BLOCK // 8):
            crowd = jnp.maximum(crowd, seen[g * 8:(g + 1) * 8])
        crowd = crowd.astype(f32)
        crowd = jnp.maximum(crowd[:, :LANES], crowd[:, LANES:])
        flags[i] = jnp.where((crowd > 3) | (degree > 4), 1.0, 0.0)
        a = place(top_ref[...], [none] * 4)
        b = place(low_ref[...], [none] * 2)
        c = place(third_ref[...], [none])
        rest = [jnp.maximum(b[0], c[0]), jnp.minimum(b[0], c[0])]
        rest = [rest[0], jnp.maximum(b[1], rest[1]), jnp.minimum(b[1], rest[1])]
        lists = sort([a[0], jnp.maximum(a[1], rest[2]), jnp.maximum(a[2], rest[1]), jnp.maximum(a[3], rest[0])])
        o_ref[:, pl.ds(pl.multiple_of(i * BLOCK, BLOCK), BLOCK)] = over_sublanes(lists)
        return carry

    lax.fori_loop(0, blocks, block_step, 0)

    most = flags[0]
    for i in range(1, blocks):
        most = jnp.maximum(most, flags[i])

    @pl.when(jnp.max(most) > 0)
    def _():
        def again(i, carry):
            @pl.when(jnp.max(flags[i]) > 0)
            def _():
                fetch(i, 0).start()
                fetch(i, 0).wait()
                planes[...] = jnp.zeros_like(planes)
                seen_ref[...] = jnp.zeros_like(seen_ref)

                def scan_chunk(c, carry):
                    a = bufs[0, :, pl.ds(pl.multiple_of(c * WIDE, WIDE), WIDE)]
                    seen_ref[...] = seen_ref[...] + a
                    x = a.astype(f32) * (c + 1).astype(f32)
                    for s in range(DEG):
                        top = planes[s].astype(f32)
                        planes[s] = jnp.maximum(top, x).astype(jnp.bfloat16)
                        x = jnp.minimum(top, x)
                    return carry

                lax.fori_loop(0, chunks, scan_chunk, 0)
                degree = lax.dot_general(ones, seen_ref[...], TURN, preferred_element_type=f32)
                lists = lax.fori_loop(0, DEG, lambda p, lists: tuple(place(planes[p], lists)), (none,) * DEG)
                o_ref[:, pl.ds(pl.multiple_of(i * BLOCK, BLOCK), BLOCK)] = jnp.where(degree > DEG, FULL, over_sublanes(list(lists)))

            return carry

        lax.fori_loop(0, blocks, again, 0)


def extract(adj_slab, half, rows):
    vertices = adj_slab.shape[1]
    tile = pltpu.VMEM((BLOCK, WIDE), jnp.bfloat16)
    return pl.pallas_call(
        extract_kernel,
        in_specs=[pl.BlockSpec(memory_space=pltpu.SMEM), pl.BlockSpec(memory_space=pl.ANY)],
        out_specs=pl.BlockSpec(memory_space=pltpu.VMEM),
        out_shape=jax.ShapeDtypeStruct((DEG, rows), f32),
        scratch_shapes=[pltpu.VMEM((READS, BLOCK, vertices), jnp.bfloat16), tile, tile, tile, tile,
                        pltpu.VMEM((DEG, BLOCK, WIDE), jnp.bfloat16), pltpu.VMEM((rows // BLOCK, 8, BLOCK), f32),
                        pltpu.SemaphoreType.DMA((READS,))],
        compiler_params=pltpu.CompilerParams(vmem_limit_bytes=40 * 1024 * 1024),
        name="extract",
    )(half, adj_slab)


def walk_kernel(lists_ref, src_ref, weight_ref, out_ref,
                table, queue, sigma, ratio, delta, cand, ids, turned, dest, tail_ref, rowhot, colhot, bins,
                ids_a, ids_b, meta, sems, *, levels, vertices, scale):
    parts, _, width = lists_ref.shape
    pitch = vertices + 8
    lane = lax.broadcasted_iota(jnp.int32, (8, LANES), 1)
    sub = lax.broadcasted_iota(jnp.int32, (8, LANES), 0)
    upper = lane >= HALF
    lane_row = lax.broadcasted_iota(jnp.int32, (1, LANES), 1)
    group_odd = ((lane_row // 32) % 2) == 1
    lane32 = lane_row % 32
    rows_all = queue.shape[0]

    def eight(row):
        return pl.ds(pl.multiple_of(row, 8), 8)

    def spread_row(ref, *index):
        return jnp.broadcast_to(ref[(*index[:-1], pl.ds(index[-1], 1), slice(None))], (8, LANES))

    srow = lax.broadcasted_iota(jnp.int32, (2 * DEG, LANES), 0)
    slane = lax.broadcasted_iota(jnp.int32, (2 * DEG, LANES), 1)

    def fill(quad):
        mine = (srow % DEG) == (slane // 32 + 4 * quad)
        pick = jnp.where(mine, jnp.where(srow < DEG, float(LANES), 1.0), 0.0).astype(jnp.bfloat16)
        per = width // SPREAD

        def body(b, most):
            x = lists_ref[b // per, :, pl.ds(pl.multiple_of(b % per * SPREAD, SPREAD), SPREAD)]
            hi = jnp.floor(x * (1.0 / LANES))
            lo = x - hi * LANES
            both = jnp.concatenate([hi, lo], axis=0).astype(jnp.bfloat16)
            table[pl.ds(pl.multiple_of(quad * pitch + b * SPREAD, 8), SPREAD), :] = lax.dot_general(
                both, pick, (((0,), (0,)), ((), ())), preferred_element_type=f32)
            for k in range(SPREAD // LANES):
                most = jnp.maximum(most, x[:, k * LANES:(k + 1) * LANES])
            return most

        most = lax.fori_loop(0, parts * per, body, jnp.full((DEG, LANES), EMPTY, f32))
        table[quad * pitch + vertices:(quad + 1) * pitch, :] = jnp.full((8, LANES), EMPTY, f32)
        return most

    most = fill(0)
    top = jnp.max(most)
    wide = jnp.max(jnp.where(sub >= 4, most, EMPTY)) >= 0
    quads = jnp.where(wide, 2, 1)

    @pl.when(wide)
    def _():
        fill(1)

    bad = top > vertices
    meta[2, 0] = bad.astype(jnp.int32)

    def clear(t, carry):
        rows = eight(t * 8)
        queue[rows, :] = jnp.full((8, LANES), -1.0, f32)
        sigma[rows, :] = jnp.zeros((8, LANES), f32)
        delta[rows, :] = jnp.zeros((8, LANES), f32)
        ids[0, rows, :] = jnp.full((8, LANES), vertices, jnp.int32)
        ids[1, rows, :] = jnp.full((8, LANES), vertices + pitch, jnp.int32)
        return carry

    lax.fori_loop(0, rows_all // 8, clear, 0)
    bins[...] = jnp.zeros_like(bins)

    def fetch(quad, row, to, which):
        return pltpu.make_async_copy(ids.at[quad, eight(row)], to, sems.at[which])

    for to, which in ((ids_a, 0), (ids_b, 1)):
        fetch(0, rows_all - 8, to, which).start()
        fetch(0, rows_all - 8, to, which).wait()

    def gather(ids_s, quad, row):
        acc = [[jnp.full((1, LANES), EMPTY, f32)] * 2 for _ in range(SLOTS)]
        for j in range(32):
            hit = lane32 == j
            for i in range(SLOTS):
                for b in range(2):
                    acc[i][b] = jnp.where(hit, table[pl.ds(ids_s[i, b * 32 + j], 1), :], acc[i][b])
        for i in range(SLOTS):
            a, b = acc[i]
            cand[2 * quad, pl.ds(row + i, 1), :] = jnp.where(group_odd, b, a)
            cand[2 * quad + 1, pl.ds(row + i, 1), :] = pltpu.roll(jnp.where(group_odd, a, b), LANES - 32, 1)

    def flag(x):
        return jnp.where(x, 1, 0)

    def level_step(level, carry):
        base, count = meta[0, level], meta[1, level]
        following = base + (count + 7) // 8 * 8
        batches = jnp.where(following <= CAP, (count + SLOTS - 1) // SLOTS, 0)
        units = batches * quads

        def at(m):
            quad = jnp.where(m >= batches, 1, 0)
            return quad, base + (m - quad * batches) * SLOTS

        def start(m, to, which):
            @pl.when(m < units)
            def _():
                fetch(*at(m), to, which).start()

        def await_(m, to, which):
            @pl.when(m < units)
            def _():
                fetch(*at(m), to, which).wait()

        def unit_step(m, to, which):
            quad, row = at(m)
            x = [cand[2 * quad + h, eight(row), :] for h in range(2)]

            def search(t, marks):
                marks = list(marks)
                for k in range(SCAN):
                    q = spread_row(queue, t * SCAN + k)
                    for h in range(2):
                        n = 2 * h + k % 2
                        marks[n] = jnp.where(x[h] == q, 1, marks[n])
                return tuple(marks)

            reach = following + meta[3, 0]
            marks = lax.fori_loop(0, (reach + SCAN - 1) // SCAN, search, (jnp.zeros((8, LANES), jnp.int32),) * 4)
            await_(m + 1, to, which)
            near = [marks[0] | marks[1] | flag(x[0] < 0), marks[2] | marks[3] | flag(x[1] < 0)]

            xr = [pltpu.roll(v, HALF, 1) for v in x]
            turns = [[(pltpu.roll(x[h], s, 0), pltpu.roll(xr[h], s, 0)) if s else (x[h], xr[h]) for s in range(8)] for h in range(2)]
            for s in range(8):
                a, b = turns[0][s]
                near[1] = jnp.where((x[1] == a) | (x[1] == b), 1, near[1])
                if s:
                    after = sub >= s
                    near[0] = jnp.where(((x[0] == a) | (x[0] == b)) & after, 1, near[0])
                    a, b = turns[1][s]
                    near[1] = jnp.where(((x[1] == a) | (x[1] == b)) & after, 1, near[1])

            new = [1 - near[0], 1 - near[1]]
            other = pltpu.roll(new[0] + 256 * new[1], HALF, 1)
            far = [other & 255, other >> 8]
            both = new[0] + 256 * new[1] + other
            run, whole = both, both
            for s in (1, 2, 4):
                run = run + jnp.where(sub >= s, pltpu.roll(run, s, 0), 0)
                whole = whole + pltpu.roll(whole, s, 0)
            run = run - both
            tail = tail_ref[...]
            begin = [tail + (run & 255), tail + (whole & 255) + (run >> 8)]
            for h in range(2):
                dest[8 * h:8 * h + 8, :] = jnp.where(new[h] > 0, begin[h] + jnp.where(upper, far[h], 0), -1)
                dest[16 + 8 * h:24 + 8 * h, :] = jnp.where(far[h] > 0, begin[h] + jnp.where(upper, 0, new[h]), -1)
                turned[8 * h:8 * h + 8, :] = xr[h]
            tail = tail + (whole & 255) + (whole >> 8)
            tail_ref[...] = tail
            length = jnp.max(tail.astype(f32)).astype(jnp.int32)

            quad2, row2 = at(jnp.minimum(m + 1, units - 1))
            gather(to, quad2, jnp.where(m + 1 < units, row2, rows_all - 8))
            start(m + 3, to, which)

            groups = (length + WINDOW - 1) // WINDOW
            fits = following + groups * WINDOW <= CAP + WINDOW
            meta[3, 0] = jnp.where(fits, length, 0)

            @pl.when(jnp.logical_not(fits))
            def _():
                meta[2, 0] = 1

            def insert(g, carry):
                slots = [eight(following + g * WINDOW + 8 * t) for t in range(WINDOW // 8)]
                qs = [queue[r, :] for r in slots]
                ss = [sigma[r, :] for r in slots]
                pos = [sub + (g * WINDOW + 8 * t) for t in range(WINDOW // 8)]
                for h in range(2):
                    for i in range(8):
                        d, e = spread_row(dest, 8 * h + i), spread_row(dest, 16 + 8 * h + i)
                        v, w = spread_row(cand, 2 * quad + h, row + i), spread_row(turned, 8 * h + i)
                        for t in range(WINDOW // 8):
                            qs[t] = jnp.where(pos[t] == d, v, jnp.where(pos[t] == e, w, qs[t]))
                for t, r in enumerate(slots):
                    queue[r, :] = qs[t]
                for i in range(8):
                    v, w = spread_row(cand, 2 * quad, row + i), spread_row(cand, 2 * quad + 1, row + i)
                    sig = spread_row(sigma, row + i)
                    for t in range(WINDOW // 8):
                        ss[t] = ss[t] + jnp.where((qs[t] == v) | (qs[t] == w), sig, 0.0)
                for t, r in enumerate(slots):
                    sigma[r, :] = ss[t]
                return carry

            lax.fori_loop(0, jnp.where(fits, groups, 0), insert, 0)

        tail_ref[...] = jnp.zeros_like(tail_ref)
        meta[3, 0] = 0
        start(0, ids_a, 0)
        start(1, ids_b, 1)

        @pl.when(units > 0)
        def _():
            fetch(0, base, ids_a, 0).wait()
            gather(ids_a, 0, base)

        start(2, ids_a, 0)

        def pair_step(p, carry):
            unit_step(2 * p, ids_b, 1)

            @pl.when(2 * p + 1 < units)
            def _():
                unit_step(2 * p + 1, ids_a, 0)

            return carry

        lax.fori_loop(0, (units + 1) // 2, pair_step, 0)

        @pl.when(following > CAP)
        def _():
            meta[2, 0] = 1

        found = jnp.where(meta[2, 0] == 0, meta[3, 0], 0)
        meta[0, level + 1] = following
        meta[1, level + 1] = found

        def settle(g, carry):
            slots = [eight(following + g * WINDOW + 8 * t) for t in range(WINDOW // 8)]
            for r in slots:
                q = queue[r, :]
                v = jnp.where(q < 0, vertices, q.astype(jnp.int32))
                ids[0, r, :] = v
                ids[1, r, :] = v + pitch
            for r in slots:
                s = sigma[r, :]
                sigma[r, :] = s + pltpu.roll(s, HALF, 1)
            return carry

        lax.fori_loop(0, (found + WINDOW - 1) // WINDOW, settle, 0)
        return carry

    @pl.when(jnp.logical_not(bad))
    def _():
        queue[0:1, :] = src_ref[...]
        sigma[0:1, :] = jnp.ones((1, LANES), f32)
        first = src_ref[...].astype(jnp.int32)
        ids[0, 0:1, :] = first
        ids[1, 0:1, :] = first + pitch
        meta[0, 0] = 0
        meta[1, 0] = 1
        lax.fori_loop(0, levels, level_step, 0)

    good = meta[2, 0] == 0

    @pl.when(good)
    def _():
        last = meta[0, levels]
        g_last = weight_ref[levels - 2]

        def seed(g, carry):
            for t in range(WINDOW // 8):
                r = eight(last + g * WINDOW + 8 * t)
                s = sigma[r, :]
                ratio[r, :] = jnp.where(s > 0, g_last / jnp.where(s > 0, s, 1.0), 0.0)
            return carry

        lax.fori_loop(0, (meta[1, levels] + WINDOW - 1) // WINDOW, seed, 0)

        def back_step(k, carry):
            level = levels - 1 - k
            base, count = meta[0, level], meta[1, level]
            nbase, ncount = meta[0, level + 1], meta[1, level + 1]
            g_here = weight_ref[jnp.maximum(level - 2, 0)]
            chunks = (ncount + 15) // 16

            def pull_batch(bt, carry):
                here = eight(base + bt * SLOTS)

                def pull_quad(quad, acc):
                    x = [cand[2 * quad + h, here, :] for h in range(2)]

                    def pull(c, acc):
                        acc = list(acc)
                        for n in range(16):
                            q = spread_row(queue, nbase + c * 16 + n)
                            w = spread_row(ratio, nbase + c * 16 + n)
                            acc[n % 2] = acc[n % 2] + jnp.where((x[0] == q) | (x[1] == q), w, 0.0)
                        return tuple(acc)

                    return lax.fori_loop(0, chunks, pull, acc)

                acc = lax.fori_loop(0, quads, pull_quad, (jnp.zeros((8, LANES), f32),) * 2)
                delta[here, :] = acc[0] + acc[1]
                return carry

            lax.fori_loop(0, (count + SLOTS - 1) // SLOTS, pull_batch, 0)

            def finish(g, carry):
                slots = [eight(base + g * WINDOW + 8 * t) for t in range(WINDOW // 8)]
                for t, r in enumerate(slots):
                    inside = g * WINDOW + 8 * t < count
                    part, s = delta[r, :], sigma[r, :]
                    d = s * (part + pltpu.roll(part, HALF, 1))
                    w = jnp.where(s > 0, (g_here + d) / jnp.where(s > 0, s, 1.0), 0.0)
                    delta[r, :] = jnp.where(inside, d, part)
                    ratio[r, :] = jnp.where(inside, w, ratio[r, :])
                return carry

            lax.fori_loop(0, (count + WINDOW - 1) // WINDOW, finish, 0)
            return carry

        lax.fori_loop(0, levels - 1, back_step, 0)

        tall = lax.broadcasted_iota(jnp.int32, (LANES, LANES), 0).astype(f32)
        start = meta[0, 1]

        def tally(t, carry):
            a, b = eight(start + t * 16), eight(start + t * 16 + 8)
            v = jnp.where(upper, queue[b, :], queue[a, :])
            d = jnp.where(upper, delta[b, :], delta[a, :])
            hi = jnp.floor(v * (1.0 / LANES))
            lo = v - hi * LANES
            d_hi = d.astype(jnp.bfloat16).astype(f32)
            d_mid = (d - d_hi).astype(jnp.bfloat16).astype(f32)
            d_lo = d - d_hi - d_mid
            for p in range(8):
                cols = slice(p * LANES, (p + 1) * LANES)
                rowhot[:, cols] = jnp.where(tall == hi[p:p + 1], 1.0, 0.0).astype(jnp.bfloat16)
                match = tall == lo[p:p + 1]
                for n, x in enumerate((d_hi, d_mid, d_lo)):
                    colhot[n * LANES:(n + 1) * LANES, cols] = jnp.where(match, x[p:p + 1], 0.0).astype(jnp.bfloat16)
            bins[...] += lax.dot_general(rowhot[...], colhot[...], TURN, preferred_element_type=f32)
            return carry

        lax.fori_loop(0, (last - start + 15) // 16, tally, 0)

    blocks = out_ref.shape[0]
    high = LANES // blocks
    total = (bins[:, :LANES] + bins[:, LANES:2 * LANES] + bins[:, 2 * LANES:]) * scale
    fault = jnp.where(good, 0.0, 1.0)
    for b in range(blocks):
        out_ref[b, 0:high, :] = total[b * high:(b + 1) * high]
        out_ref[b, high:, :] = jnp.full((8, LANES), fault, f32)


def walk(lists, src_row, weights, *, blocks, vertices, scale):
    levels = weights.shape[0] + 1
    rows = CAP + 4 * WINDOW
    high = LANES // blocks + 8
    vm = pltpu.VMEM
    queue = vm((rows, LANES), f32)
    return pl.pallas_call(
        functools.partial(walk_kernel, levels=levels, vertices=vertices, scale=scale),
        in_specs=[pl.BlockSpec(memory_space=pltpu.VMEM), pl.BlockSpec(memory_space=pltpu.VMEM), pl.BlockSpec(memory_space=pltpu.SMEM)],
        out_specs=pl.BlockSpec(memory_space=pltpu.VMEM),
        out_shape=jax.ShapeDtypeStruct((blocks, high, LANES), f32),
        scratch_shapes=[
            vm((2 * (vertices + 8), LANES), f32), queue, queue, queue, queue,
            vm((4, rows, LANES), f32), vm((2, rows, LANES), jnp.int32),
            vm((16, LANES), f32), vm((32, LANES), jnp.int32), vm((8, LANES), jnp.int32),
            vm((LANES, 8 * LANES), jnp.bfloat16), vm((3 * LANES, 8 * LANES), jnp.bfloat16), vm((LANES, 3 * LANES), f32),
            pltpu.SMEM((SLOTS, LANES), jnp.int32), pltpu.SMEM((SLOTS, LANES), jnp.int32), pltpu.SMEM((4, 16), jnp.int32),
            pltpu.SemaphoreType.DMA((2,)),
        ],
        compiler_params=pltpu.CompilerParams(vmem_limit_bytes=48 * 1024 * 1024),
        name="walk",
    )(lists, src_row, weights)


def everyone(src, graph):
    return [(y, g) for y in range(src) for g in range(graph)]


def meet(peers):
    barrier = pltpu.get_barrier_semaphore()
    for y, g in peers:
        pl.semaphore_signal(barrier, inc=1, device_id={"src": y, "graph": g}, device_id_type=MESH)
    pl.semaphore_wait(barrier, len(peers))


def share_kernel(src, graph, x_ref, o_ref, own_sem, send_sem, recv_sem):
    y, g = lax.axis_index("src"), lax.axis_index("graph")
    others = [((y + i) % src, (g + k) % graph) for i, k in everyone(src, graph)][1:]
    meet(others)
    mine = g * src + y
    own = pltpu.make_async_copy(x_ref, o_ref.at[mine], own_sem)
    own.start()
    copies = []
    for n, (py, pg) in enumerate(others):
        copies.append(pltpu.make_async_remote_copy(
            src_ref=x_ref, dst_ref=o_ref.at[mine], send_sem=send_sem.at[n], recv_sem=recv_sem.at[n],
            device_id={"src": py, "graph": pg}, device_id_type=MESH))
        copies[-1].start()
    own.wait()
    for c in copies:
        c.wait()


def share(x, src, graph):
    n = src * graph
    return pl.pallas_call(
        functools.partial(share_kernel, src, graph),
        in_specs=[pl.BlockSpec(memory_space=pltpu.VMEM)],
        out_specs=pl.BlockSpec(memory_space=pltpu.VMEM),
        out_shape=jax.ShapeDtypeStruct((n,) + x.shape, x.dtype),
        scratch_shapes=[pltpu.SemaphoreType.DMA, pltpu.SemaphoreType.DMA((n - 1,)), pltpu.SemaphoreType.DMA((n - 1,))],
        compiler_params=pltpu.CompilerParams(collective_id=0, has_side_effects=True),
        name="share",
    )(x)


def total_kernel(src, graph, x_ref, o_ref, got, own_sem, send_sem, recv_sem):
    y, g = lax.axis_index("src"), lax.axis_index("graph")
    others = [((y + i) % src, (g + k) % graph) for i, k in everyone(src, graph)][1:]
    meet(others)
    mine = g * src + y
    own = pltpu.make_async_copy(x_ref.at[g], got.at[mine], own_sem)
    own.start()
    copies = []
    for n, (py, pg) in enumerate(others):
        copies.append(pltpu.make_async_remote_copy(
            src_ref=x_ref.at[pg], dst_ref=got.at[mine], send_sem=send_sem.at[n], recv_sem=recv_sem.at[n],
            device_id={"src": py, "graph": pg}, device_id_type=MESH))
        copies[-1].start()
    own.wait()
    for c in copies:
        c.wait()
    acc = got[0]
    for n in range(1, src * graph):
        acc = acc + got[n]
    o_ref[...] = acc


def total(x, src, graph):
    n = src * graph
    return pl.pallas_call(
        functools.partial(total_kernel, src, graph),
        in_specs=[pl.BlockSpec(memory_space=pltpu.VMEM)],
        out_specs=pl.BlockSpec(memory_space=pltpu.VMEM),
        out_shape=jax.ShapeDtypeStruct(x.shape[1:], x.dtype),
        scratch_shapes=[pltpu.VMEM((n,) + x.shape[1:], x.dtype), pltpu.SemaphoreType.DMA,
                        pltpu.SemaphoreType.DMA((n - 1,)), pltpu.SemaphoreType.DMA((n - 1,))],
        compiler_params=pltpu.CompilerParams(collective_id=1, has_side_effects=True),
        name="total",
    )(x)


def dense(adj_slab, src_local, level_weight, src, graph):
    slab_rows, vertex_count = adj_slab.shape
    src_count = src_local.shape[0]
    levels = level_weight.shape[0] + 1
    row_start = lax.axis_index("graph") * slab_rows
    vertex_ids = row_start + lax.broadcasted_iota(jnp.int32, (slab_rows, 1), 0)
    first = jnp.where(vertex_ids == src_local[None, :], 1.0, 0.0).astype(f32)

    def forward(carry, unused):
        sigma, seen = carry
        partial = jnp.einsum("uv,us->vs", adj_slab, sigma, preferred_element_type=f32, precision=exact_precision)
        parts = lax.all_to_all(partial.reshape(graph, slab_rows, src_count), "graph", 0, 0)
        sigma = jnp.sum(parts, axis=0) * (1.0 - seen)
        seen = jnp.maximum(seen, jnp.where(sigma > 0, 1.0, 0.0))
        return (sigma, seen), sigma

    _, sigmas = lax.scan(forward, (first, first), None, length=levels)

    def backward(carry, xs):
        delta, acc = carry
        upper, lower, weight = xs
        reached = upper > 0
        ratio = jnp.where(reached, (weight + delta) / jnp.where(reached, upper, 1.0), 0.0)
        gathered = lax.all_to_all(jnp.broadcast_to(ratio[None], (graph,) + ratio.shape), "graph", 0, 0)
        pulled = jnp.einsum("uv,vs->us", adj_slab, gathered.reshape(vertex_count, src_count),
                            preferred_element_type=f32, precision=exact_precision)
        delta = lower * pulled
        return (delta, acc + delta), None

    zero = jnp.zeros_like(first)
    (_, acc), _ = lax.scan(backward, (zero, zero), (sigmas[1:][::-1], sigmas[:-1][::-1], level_weight[::-1]))
    scale = vertex_count / (src_count * src * levels ** 3)
    mine = jnp.sum(acc, axis=1) * scale
    both = lax.all_to_all(jnp.broadcast_to(mine.reshape(1, -1, LANES), (src, slab_rows // LANES, LANES)), "src", 0, 0)
    return jnp.sum(both, axis=0).reshape(slab_rows)


def solution(mesh):
    src, graph = mesh.shape["src"], mesh.shape["graph"]

    def device_program(adj_slab, src_local, level_weight):
        slab_rows, vertex_count = adj_slab.shape
        levels = level_weight.shape[0] + 1
        half = lax.axis_index("src").astype(jnp.int32).reshape(1)
        lists = share(extract(adj_slab, half, slab_rows // src), src, graph)
        mine = lax.dynamic_slice(src_local, (lax.axis_index("graph") * HALF,), (HALF,)).astype(f32)
        scale = vertex_count / (HALF * src * graph * levels ** 3)
        parts = walk(lists, jnp.concatenate([mine, mine])[None], level_weight, blocks=graph, vertices=vertex_count, scale=scale)
        summed = total(parts, src, graph)
        high = slab_rows // LANES
        return lax.cond(summed[high, 0] > 0,
                        lambda: dense(adj_slab, src_local, level_weight, src, graph),
                        lambda: summed[:high].reshape(slab_rows))

    return jax.shard_map(device_program, mesh=mesh,
                         in_specs=(P(("batch", "graph"), None), P(("batch", "src")), P(None)),
                         out_specs=P(("batch", "graph")), check_vma=False)
```

time: 170 us -> 103 us (0.61)
  Pallas kernels: 165 us -> 98.2 us
    pallas_call x1, Pallas kernels: 102 us -> 55.6 us  [walk(): pl.pallas_call(functools.partial(walk_kernel, levels=levels, vertices=ver...]
    pallas_call x1, Pallas kernels: 23.7 us -> 12.4 us  [share(): pl.pallas_call(functools.partial(share_kernel, src, graph), in_specs=[pl....]
    pallas_call x1, Pallas kernels: 32.7 us -> 23.2 us  [extract(): pl.pallas_call(extract_kernel, in_specs=[pl.BlockSpec(memory_space=pltpu....]
where the time goes in v2:
time: 103 us
  Pallas kernels  98.2 us (95%)
  local copies, waits for them, and re-layouts  3.4 us (3%)
    pallas_call x1, Pallas kernels, walk(): pl.pallas_call(functools.partial(walk_kernel, levels=levels, vertices=ver...  55.6 us
    pallas_call x1, Pallas kernels, extract(): pl.pallas_call(extract_kernel, in_specs=[pl.BlockSpec(memory_space=pltpu....  23.2 us
    pallas_call x1, Pallas kernels, share(): pl.pallas_call(functools.partial(share_kernel, src, graph), in_specs=[pl....  12.4 us
    pallas_call x1, Pallas kernels, total(): pl.pallas_call(functools.partial(total_kernel, src, graph), in_specs=[pl....  6.93 us
    unnamed x10, local copies, waits for them, and re-layouts  2.28 us

profile of v2, /device:TPU:0, one launch (start us, length us, event | category | flops | bytes accessed | tf_op | source)
XLA Modules:
  0.0 103.2 jit_solution(2383849911198339772)
XLA Ops:
  0.0 0.8 dynamic-slice_convert_fusion
  0.8 0.1 maximum_bitcast_fusion.src_ref
  0.8 0.0 copy-start.5
  0.8 0.0 copy-start.4
  0.8 23.2 %extract.1.x_ref = f32[8,2048]{1,0:T(8,128)S(1)} custom-call(s32[1]{0:T(128)} %bitcast.5.half_ref, bf16[4096,16384]{1,0:T(8,128)(2,1)} %a_ref.1), custom_call_target="tpu_custom_call" | custom-call | tf_op jit(solution)/shard_map/extract/pallas_call | solution.py:171
  24.0 0.0 copy-start.2
  24.0 0.6 copy-done.2
  24.7 12.4 %share.1.lists_ref = f32[8,8,2048]{2,1,0:T(8,128)} custom-call(f32[8,2048]{1,0:T(8,128)} %copy-done.2), custom_call_target="tpu_custom_call" | custom-call | tf_op jit(solution)/shard_map/share/pallas_call | solution.py:581
  37.1 0.0 copy-done.5
  37.1 0.0 copy-start
  37.1 1.0 %copy-done = f32[8,8,2048]{2,1,0:T(8,128)S(1)} copy-done((f32[8,8,2048]{2,1,0:T(8,128)S(1)}, f32[8,8,2048]{2,1,0:T(8,128)}, u32[]{:S(2)}) %copy-start) | copy-done | bytes 524312
  38.2 55.6 %walk.1.x_ref = f32[4,40,128]{2,1,0:T(8,128)S(1)} custom-call(f32[8,8,2048]{2,1,0:T(8,128)S(1)} %copy-done, f32[1,128]{1,0:T(1,128)S(1)} %maximum_bitcast_fusion.src_ref, f32[11]{0:T(128)S(1)} %copy-done.5), custom_call_target="tpu_custom_call" | custom-call | tf_op jit(solution)/shard_map/walk/pallas_call | solution.py:532
  93.8 0.0 copy-start.1
  93.8 0.6 copy-done.1
  94.4 6.9 %total.1 = f32[40,128]{1,0:T(8,128)S(1)} custom-call(f32[4,40,128]{2,1,0:T(8,128)} %copy-done.1), custom_call_target="tpu_custom_call" | custom-call | tf_op jit(solution)/shard_map/total/pallas_call | solution.py:616
  101.4 0.5 slice.12
  102.5 0.0 copy-done.4
  102.6 0.6 conditional.1
  102.6 0.6 slice_bitcast_fusion
Async XLA Ops:
  0.8 36.3 %copy-start.5 = (f32[11]{0:T(128)S(1)}, f32[11]{0:T(128)}, u32[]{:S(2)}) copy-start(f32[11]{0:T(128)} %weight_ref.1) | copy-start | bytes 136
  0.8 101.7 %copy-start.4 = (s32[256]{0:T(256)S(1)}, s32[256]{0:T(256)}, u32[]{:S(2)}) copy-start(s32[256]{0:T(256)} %param.10) | copy-start | bytes 3076
  24.0 0.6 copy-start.2
  37.1 1.0 %copy-start = (f32[8,8,2048]{2,1,0:T(8,128)S(1)}, f32[8,8,2048]{2,1,0:T(8,128)}, u32[]{:S(2)}) copy-start(f32[8,8,2048]{2,1,0:T(8,128)} %share.1.lists_ref) | copy-start | bytes 1572868
  93.8 0.6 copy-start.1
